TPU v7x, 32 devices: a whole 2x2x4 slice. The times are simulated.
32 devices in a mesh: group: 4 (over y, x), fsdp: 2 (over core), tensor: 4 (over z).
Axes of the slice: x: 2, y: 2, z: 4, core: 2. Of those that a mesh axis runs over, the one named last changes fastest.
Arguments:
- patches: bfloat16 [4, 2, 8, 577, 1024], P('group', None, ('fsdp', 'tensor')), may hold values from -6 to 6
- output_grad: bfloat16 [4, 2, 8, 577, 1024], P('group', None, ('fsdp', 'tensor')), may hold values from -6 to 6
- live_counts: int32 [4, 2, 2], P('group'), may hold values from 1 to 4, as said below
- attn_master: float32 [4, 1024, 1024], P(None, 'fsdp', 'tensor')
- mlp_master: float32 [2, 1024, 4096], P(None, 'fsdp', 'tensor')
- vector_master: float32 [12, 1024], replicated
- attn_moments: float32 [4, 2, 4, 1024, 1024], P('group', None, None, 'fsdp', 'tensor'), as said below
- mlp_moments: float32 [4, 2, 2, 1024, 4096], P('group', None, None, 'fsdp', 'tensor'), as said below
- vector_moments: float32 [4, 2, 12, 1024], P('group'), as said below
- attn_outer: float32 [4, 1024, 1024], P(None, 'fsdp', 'tensor'), may hold values from -0.125 to 0.125
- mlp_outer: float32 [2, 1024, 4096], P(None, 'fsdp', 'tensor'), may hold values from -0.125 to 0.125
- vector_outer: float32 [12, 1024], replicated, may hold values from -0.625 to 0.625
Outputs:
- block_output: bfloat16 [4, 2, 8, 577, 1024], P('group', None, ('fsdp', 'tensor'))
- patches_grad: float32 [4, 2, 8, 577, 1024], P('group', None, ('fsdp', 'tensor'))
- attn_inner: float32 [4, 2, 4, 1024, 1024], P('group', None, None, 'fsdp', 'tensor')
- attn_state: float32 [3, 4, 1024, 1024], P(None, None, 'fsdp', 'tensor')
- attn_copy: bfloat16 [4, 1024, 1024], P(None, 'fsdp', 'tensor')
- mlp_inner: float32 [4, 2, 2, 1024, 4096], P('group', None, None, 'fsdp', 'tensor')
- mlp_state: float32 [3, 2, 1024, 4096], P(None, None, 'fsdp', 'tensor')
- mlp_copy: bfloat16 [2, 1024, 4096], P(None, 'fsdp', 'tensor')
- vector_inner: float32 [4, 2, 12, 1024], P('group')
- vector_state: float32 [3, 12, 1024], replicated
- vector_copy: bfloat16 [12, 1024], replicated
Inputs may be any that keep to these rules, and one draw needn't show every extreme that they name: live_counts[g, m, f] images are live, and they stand first, among the f-th block of 4 image slots of micro-batch m in group g; some entry equals 4. `attn_moments`: second moments are positive. `mlp_moments`: second moments are positive. `vector_moments`: second moments are positive.
All inputs are finite; a program needn't handle non-finite values.
Results may differ from a plain program's by a relative error of at most 0.012.
The roundings to bfloat16 on the way count: a program that leaves them out, or rounds other values in their place, can miss the bound.
Values may be sent and summed in bfloat16 or wider, within the bound.
A program may use at most 320 MiB of HBM per device.

v0:
```python
from functools import partial
import jax
import jax.numpy as jnp
from jax import lax
from jax.sharding import PartitionSpec as P

HD = 64
FF = 4096
STEP = 8
EPSILON = 1e-06
INNER_RATE = 0.02
VECTOR_RATE = 0.2
WEIGHT_DECAY = 0.1
OUTER_RATE = 0.7
OUTER_MOMENTUM = 0.9


def normalize(source, gain_row, shift_row):
    centre = source - jnp.mean(source, axis=-1, keepdims=True)
    spread = jnp.mean(centre * centre, axis=-1, keepdims=True)
    return centre * lax.rsqrt(spread + EPSILON) * gain_row + shift_row


def gelu_exact(source):
    return jax.nn.gelu(source, approximate=False)


def gelu_slope(source):
    return (
        0.5 * (1.0 + lax.erf(source * 0.7071067811865476))
        + source * jnp.exp(-0.5 * source * source) * 0.3989422804014327
    )


def inner_adamw(master, gradient, moments, step_rate, decay_rate):
    first_moment = 0.9 * moments[0] + 0.1 * gradient
    second_moment = 0.95 * moments[1] + 0.05 * gradient * gradient
    step_ratio = (
        first_moment / (1.0 - 0.9**STEP) / (jnp.sqrt(second_moment / (1.0 - 0.95**STEP)) + 1e-08)
    )
    return (master - step_rate * (step_ratio + decay_rate * master), second_moment)


def outer_nesterov(master, outer_old, difference):
    momentum = OUTER_MOMENTUM * outer_old + difference
    updated = master - OUTER_RATE * (difference + OUTER_MOMENTUM * momentum)
    return (jnp.stack([difference, momentum, updated]), updated.astype(jnp.bfloat16))


def attend_forward(score_scale, operands):
    queries_low, keys_low, values_low = operands
    scores = (
        jnp.einsum("qhe,khe->hqk", queries_low, keys_low, preferred_element_type=jnp.float32)
        * score_scale
    )
    highest = jnp.max(scores, axis=-1, keepdims=True)
    exponent = jnp.exp(scores - highest)
    totals = jnp.sum(exponent, axis=-1, keepdims=True)
    probs_low = (exponent / totals).astype(jnp.bfloat16)
    attended = jnp.einsum("hqk,khe->qhe", probs_low, values_low, preferred_element_type=jnp.float32)
    return (attended.astype(jnp.bfloat16), (highest + jnp.log(totals))[..., 0])


def attend_backward(score_scale, operands):
    queries_low, keys_low, values_low, log_totals, grad_attended = operands
    scores = (
        jnp.einsum("qhe,khe->hqk", queries_low, keys_low, preferred_element_type=jnp.float32)
        * score_scale
    )
    probs_full = jnp.exp(scores - log_totals[..., None])
    grad_probs = jnp.einsum(
        "qhe,khe->hqk", grad_attended, values_low, preferred_element_type=jnp.float32
    )
    grad_values = jnp.einsum(
        "hqk,qhe->khe",
        probs_full.astype(jnp.bfloat16),
        grad_attended,
        preferred_element_type=jnp.float32,
    )
    weighted = jnp.sum(probs_full * grad_probs, axis=-1, keepdims=True)
    grad_scores = (probs_full * (grad_probs - weighted)).astype(jnp.bfloat16)
    grad_queries = (
        jnp.einsum("hqk,khe->qhe", grad_scores, keys_low, preferred_element_type=jnp.float32)
        * score_scale
    )
    grad_keys = (
        jnp.einsum("hqk,qhe->khe", grad_scores, queries_low, preferred_element_type=jnp.float32)
        * score_scale
    )
    return (
        grad_queries.astype(jnp.bfloat16),
        grad_keys.astype(jnp.bfloat16),
        grad_values.astype(jnp.bfloat16),
    )


def local(
    patches,
    output_grad,
    live_counts,
    attn_master,
    mlp_master,
    vector_master,
    attn_moments,
    mlp_moments,
    vector_moments,
    attn_outer,
    mlp_outer,
    vector_outer,
):
    narrow = jnp.bfloat16
    single = jnp.float32
    tensor_index = lax.axis_index("tensor")
    fsdp_index = lax.axis_index("fsdp")
    micro_count = patches.shape[1]
    local_images = patches.shape[2]
    seq_len = patches.shape[3]
    width = patches.shape[4]
    head_cols = attn_master.shape[2]
    hidden_cols = mlp_master.shape[2]
    score_scale = HD ** (-0.5)
    attn_all, mlp_all = (
        lax.all_gather(attn_master.astype(narrow), "fsdp", axis=1, tiled=True),
        lax.all_gather(mlp_master.astype(narrow), "fsdp", axis=1, tiled=True),
    )
    bias_query = lax.dynamic_slice_in_dim(vector_master[4], tensor_index * head_cols, head_cols)
    bias_value = lax.dynamic_slice_in_dim(vector_master[5], tensor_index * head_cols, head_cols)
    head_width = attn_all.shape[2]
    heads_here = head_width // HD
    bias_hidden = lax.dynamic_slice_in_dim(
        vector_master[8:].reshape(-1), tensor_index * hidden_cols, hidden_cols
    )
    owner_counts = jnp.sum(
        jnp.where(jnp.arange(live_counts.shape[2]) == fsdp_index, live_counts[0], 0), axis=-1
    )
    slot_index = tensor_index * local_images + jnp.arange(local_images)
    alive_all = (slot_index[None, :] < owner_counts[:, None]).astype(single)
    forward_attend = partial(attend_forward, score_scale)
    backward_attend = partial(attend_backward, score_scale)
    qkv_acc = jnp.zeros((3, width, head_width), single)
    out_acc = jnp.zeros((width, head_width), single)
    fc_in_acc = jnp.zeros((width, hidden_cols), single)
    fc_out_acc = jnp.zeros((width, hidden_cols), single)
    hidden_bias_acc = jnp.zeros((hidden_cols,), single)
    query_bias_acc = jnp.zeros((head_width,), single)
    value_bias_acc = jnp.zeros((head_width,), single)
    vector_acc = jnp.zeros((6, width), single)
    outputs_mixed = []
    outputs_grad = []
    for batch_index in range(micro_count):
        inputs = patches[0, batch_index].astype(single)
        alive = alive_all[batch_index][:, None, None]
        normed_one = normalize(inputs, vector_master[0], vector_master[1]).astype(narrow)
        rows_attn = lax.all_gather(normed_one, "tensor", axis=0, tiled=True)
        image_count = rows_attn.shape[0]
        shape_heads = (image_count, seq_len, heads_here, HD)
        projected = jnp.einsum(
            "isd,jde->jise", rows_attn, attn_all[:3], preferred_element_type=single
        )
        queries_low = (projected[0] + bias_query).astype(narrow).reshape(shape_heads)
        keys_low = projected[1].astype(narrow).reshape(shape_heads)
        values_low = (projected[2] + bias_value).astype(narrow).reshape(shape_heads)
        attended, log_totals = lax.map(forward_attend, (queries_low, keys_low, values_low))
        attended = attended.reshape(image_count, seq_len, head_width)
        branch_one = lax.psum_scatter(
            jnp.einsum("ise,de->isd", attended, attn_all[3], preferred_element_type=single),
            "tensor",
            scatter_dimension=0,
            tiled=True,
        )
        resid_one = inputs + branch_one + vector_master[6]
        normed_two = normalize(resid_one, vector_master[2], vector_master[3]).astype(narrow)
        rows_mlp = lax.all_gather(normed_two, "tensor", axis=0, tiled=True)
        pre_act = (
            jnp.einsum("isd,df->isf", rows_mlp, mlp_all[0], preferred_element_type=single)
            + bias_hidden
        )
        hidden = gelu_exact(pre_act).astype(narrow)
        branch_two = lax.psum_scatter(
            jnp.einsum("isf,df->isd", hidden, mlp_all[1], preferred_element_type=single),
            "tensor",
            scatter_dimension=0,
            tiled=True,
        )
        outputs_mixed.append((alive * (resid_one + branch_two + vector_master[7])).astype(narrow))
        grad_out = alive * output_grad[0, batch_index].astype(single)
        rows_grad_two = lax.all_gather(grad_out.astype(narrow), "tensor", axis=0, tiled=True)
        fc_out_acc = fc_out_acc + jnp.einsum(
            "isd,isf->df", rows_grad_two, hidden, preferred_element_type=single
        )
        grad_hidden = jnp.einsum(
            "isd,df->isf", rows_grad_two, mlp_all[1], preferred_element_type=single
        )
        grad_pre = (grad_hidden * gelu_slope(pre_act)).astype(narrow)
        fc_in_acc = fc_in_acc + jnp.einsum(
            "isd,isf->df", rows_mlp, grad_pre, preferred_element_type=single
        )
        hidden_bias_acc = hidden_bias_acc + jnp.sum(grad_pre.astype(single), axis=(0, 1))
        grad_normed_two = lax.psum_scatter(
            jnp.einsum("isf,df->isd", grad_pre, mlp_all[0], preferred_element_type=single),
            "tensor",
            scatter_dimension=0,
            tiled=True,
        )
        unused_two, norm_pull_two = jax.vjp(
            normalize, resid_one, vector_master[2], vector_master[3]
        )
        back_resid, gain_two, shift_two = norm_pull_two(grad_normed_two)
        grad_resid = grad_out + back_resid
        rows_grad_one = lax.all_gather(grad_resid.astype(narrow), "tensor", axis=0, tiled=True)
        out_acc = out_acc + jnp.einsum(
            "isd,ise->de", rows_grad_one, attended, preferred_element_type=single
        )
        grad_attended = jnp.einsum(
            "isd,de->ise", rows_grad_one, attn_all[3], preferred_element_type=single
        ).astype(narrow)
        grad_queries, grad_keys, grad_values = lax.map(
            backward_attend,
            (queries_low, keys_low, values_low, log_totals, grad_attended.reshape(shape_heads)),
        )
        grad_queries = grad_queries.reshape(image_count, seq_len, head_width)
        grad_keys = grad_keys.reshape(image_count, seq_len, head_width)
        grad_values = grad_values.reshape(image_count, seq_len, head_width)
        grad_stack = jnp.stack([grad_queries, grad_keys, grad_values])
        qkv_acc = qkv_acc + jnp.einsum(
            "isd,jise->jde", rows_attn, grad_stack, preferred_element_type=single
        )
        query_bias_acc = query_bias_acc + jnp.sum(grad_queries.astype(single), axis=(0, 1))
        value_bias_acc = value_bias_acc + jnp.sum(grad_values.astype(single), axis=(0, 1))
        summed = jnp.einsum("ise,de->isd", grad_queries, attn_all[0], preferred_element_type=single)
        summed = summed + jnp.einsum(
            "ise,de->isd", grad_keys, attn_all[1], preferred_element_type=single
        )
        grad_normed_one = lax.psum_scatter(
            summed
            + jnp.einsum("ise,de->isd", grad_values, attn_all[2], preferred_element_type=single),
            "tensor",
            scatter_dimension=0,
            tiled=True,
        )
        unused_one, norm_pull_one = jax.vjp(normalize, inputs, vector_master[0], vector_master[1])
        back_inputs, gain_one, shift_one = norm_pull_one(grad_normed_one)
        outputs_grad.append(grad_resid + back_inputs)
        vector_acc = vector_acc + jnp.stack(
            [
                gain_one,
                shift_one,
                gain_two,
                shift_two,
                jnp.sum(grad_resid, axis=(0, 1)),
                jnp.sum(grad_out, axis=(0, 1)),
            ]
        )
    attn_grad_full = jnp.concatenate([qkv_acc, out_acc[None]], 0)
    query_row = lax.dynamic_update_slice_in_dim(
        jnp.zeros((width,), single), query_bias_acc, tensor_index * head_cols, 0
    )
    value_row = lax.dynamic_update_slice_in_dim(
        jnp.zeros((width,), single), value_bias_acc, tensor_index * head_cols, 0
    )
    mlp_grad_cols = jnp.stack([fc_in_acc, fc_out_acc])
    attn_grad, mlp_grad = (
        lax.psum_scatter(attn_grad_full, "fsdp", scatter_dimension=1, tiled=True),
        lax.psum_scatter(mlp_grad_cols, "fsdp", scatter_dimension=1, tiled=True),
    )
    hidden_rows = lax.dynamic_update_slice_in_dim(
        jnp.zeros((FF,), single), hidden_bias_acc, tensor_index * hidden_cols, 0
    ).reshape(-1, width)
    vector_part = jnp.concatenate(
        [vector_acc[:4], jnp.stack([query_row, value_row]), vector_acc[4:], hidden_rows], 0
    )
    vector_grad = lax.psum(vector_part, ("fsdp", "tensor"))
    new_attn, second_attn = inner_adamw(
        attn_master, attn_grad, attn_moments[0], INNER_RATE, WEIGHT_DECAY
    )
    new_mlp, second_mlp = inner_adamw(
        mlp_master, mlp_grad, mlp_moments[0], INNER_RATE, WEIGHT_DECAY
    )
    new_vector, second_vector = inner_adamw(
        vector_master, vector_grad, vector_moments[0], VECTOR_RATE, 0.0
    )
    diff_attn, diff_mlp, diff_vector = lax.psum(
        (attn_master - new_attn, mlp_master - new_mlp, vector_master - new_vector), "group"
    )
    groups = lax.axis_size("group")
    attn_state, attn_copy = outer_nesterov(attn_master, attn_outer, diff_attn / groups)
    mlp_state, mlp_copy = outer_nesterov(mlp_master, mlp_outer, diff_mlp / groups)
    vector_state, vector_copy = outer_nesterov(vector_master, vector_outer, diff_vector / groups)
    block_output = jnp.stack(outputs_mixed)[None]
    patches_grad = jnp.stack(outputs_grad)[None]
    attn_inner = jnp.stack([attn_grad, second_attn])[None]
    mlp_inner = jnp.stack([mlp_grad, second_mlp])[None]
    vector_inner = jnp.stack([vector_grad, second_vector])[None]
    return (
        block_output,
        patches_grad,
        attn_inner,
        attn_state,
        attn_copy,
        mlp_inner,
        mlp_state,
        mlp_copy,
        vector_inner,
        vector_state,
        vector_copy,
    )


def solution(mesh):
    placed = (
        P("group", None, ("fsdp", "tensor"), None, None),
        P("group", None, ("fsdp", "tensor"), None, None),
        P("group", None, None),
        P(None, "fsdp", "tensor"),
        P(None, "fsdp", "tensor"),
        P(),
        P("group", None, None, "fsdp", "tensor"),
        P("group", None, None, "fsdp", "tensor"),
        P("group", None, None, None),
        P(None, "fsdp", "tensor"),
        P(None, "fsdp", "tensor"),
        P(),
    )
    return jax.shard_map(
        local,
        mesh=mesh,
        in_specs=placed,
        out_specs=(
            P("group", None, ("fsdp", "tensor"), None, None),
            P("group", None, ("fsdp", "tensor"), None, None),
            P("group", None, None, "fsdp", "tensor"),
            P(None, None, "fsdp", "tensor"),
            P(None, "fsdp", "tensor"),
            P("group", None, None, "fsdp", "tensor"),
            P(None, None, "fsdp", "tensor"),
            P(None, "fsdp", "tensor"),
            P("group", None, None, None),
            P(),
            P(),
        ),
        check_vma=False,
    )
```

profile of v0, /device:TPU:0, one launch (start us, length us, event | category | flops | bytes accessed | tf_op | source)
XLA Modules:
  0.0 2521.2 jit_solution(1555532051777853854)
XLA Ops:
  23.5 93.8 %all-gather.19.cloned.1.call-done = bf16[4,577,1024]{2,1,0:T(8,128)(2,1)} async-done(((bf16[1,577,1024]{2,1,0:T(8,128)(2,1)}), bf16[4,577,1024]{2,1,0:T(8,128)(2,1)}) %all-gather.19.cloned.1.call-update) | async-done | bytes 4726800 | tf_op jit(solution)/shard_map/all_gather | solution.py:154
  126.6 81.9 %all-gather.11.cloned.1.call-done = bf16[4,577,1024]{2,1,0:T(8,128)(2,1)} async-done(((bf16[1,577,1024]{2,1,0:T(8,128)(2,1)}), bf16[4,577,1024]{2,1,0:T(8,128)(2,1)}) %all-gather.11.cloned.1.call-update) | async-done | bytes 4726800 | tf_op jit(solution)/shard_map/all_gather | solution.py:154
  240.4 25.3 %while.53 = (s32[]{:T(128)}, bf16[4,577,4,64]{1,3,2,0:T(8,128)(2,1)}, f32[4,4,577]{2,1,0:T(4,128)S(1)}, bf16[4,577,4,64]{1,3,2,0:T(8,128)(2,1)}, bf16[4,577,4,64...) while((s32[]{:T(128)}, bf16[4,577,4,64]{1,3,2,0:T(8,128)(2,1)}, ...), condition=%wide.region_16.17_spmd, body=%wide.region_13.16_spmd.sunk | while | flops 353050112 | bytes 17370320 | solution.py:163
  265.8 7.3 fusion.237
  279.1 21.4 while.52
  300.5 7.9 fusion.238
  312.4 122.7 %reduce-scatter.15.cloned.1.call-done = f32[1,577,1024]{2,1,0:T(8,128)} async-done(((f32[4,577,1024]{2,1,0:T(8,128)}), f32[1,577,1024]{2,1,0:T(8,128)}) %reduce-scatter.15.cloned.1.call-update) | async-done | bytes 2363408 | tf_op jit(solution)/shard_map/reduce_scatter | solution.py:165
  435.1 167.2 %reduce-scatter.11.cloned.1.call-done = f32[1,577,1024]{2,1,0:T(8,128)} async-done(((f32[4,577,1024]{2,1,0:T(8,128)}), f32[1,577,1024]{2,1,0:T(8,128)}) %reduce-scatter.11.cloned.1.call-update) | async-done | bytes 2363408 | tf_op jit(solution)/shard_map/reduce_scatter | solution.py:165
  610.7 8.6 fusion.279
  629.3 83.4 %all-gather.21.cloned.1.call-done = bf16[4,577,1024]{2,1,0:T(8,128)(2,1)} async-done(((bf16[1,577,1024]{2,1,0:T(8,128)(2,1)}), bf16[4,577,1024]{2,1,0:T(8,128)(2,1)}) %all-gather.21.cloned.1.call-update) | async-done | bytes 4726800 | tf_op jit(solution)/shard_map/all_gather | solution.py:173
  712.7 10.2 fusion.225
  722.9 80.9 %all-gather.15.cloned.1.call-done = bf16[4,577,1024]{2,1,0:T(8,128)(2,1)} async-done(((bf16[1,577,1024]{2,1,0:T(8,128)(2,1)}), bf16[4,577,1024]{2,1,0:T(8,128)(2,1)}) %all-gather.15.cloned.1.call-update) | async-done | bytes 4726800 | tf_op jit(solution)/shard_map/all_gather | solution.py:173
  803.8 20.2 fusion.210
  824.0 70.3 %all-gather.23.cloned.1.call-done = bf16[4,577,1024]{2,1,0:T(8,128)(2,1)} async-done(((bf16[1,577,1024]{2,1,0:T(8,128)(2,1)}), bf16[4,577,1024]{2,1,0:T(8,128)(2,1)}) %all-gather.23.cloned.1.call-update) | async-done | bytes 4726800 | tf_op jit(solution)/shard_map/all_gather | solution.py:187
  894.3 12.3 convert_reduce_fusion.1
  908.8 8.0 fusion.224
  917.0 67.8 %all-gather.27.cloned.1.call-done = bf16[4,577,1024]{2,1,0:T(8,128)(2,1)} async-done(((bf16[1,577,1024]{2,1,0:T(8,128)(2,1)}), bf16[4,577,1024]{2,1,0:T(8,128)(2,1)}) %all-gather.27.cloned.1.call-update) | async-done | bytes 4726800 | tf_op jit(solution)/shard_map/all_gather | solution.py:187
  984.7 12.5 convert_reduce_fusion
  999.4 7.6 fusion.223
  1007.1 46.6 %fusion.116 = (bf16[4,577,1024]{2,1,0:T(8,128)(2,1)S(1)}, bf16[4,577,1024]{2,1,0:T(8,128)(2,1)}) fusion(f32[4,577,1024]{2,1,0:T(8,128)} %get-tuple-element.421, f32[1024]{0:T(1024)S(1)} %dynamic_slice.61, u8[577,1024]{1,0:T(8,128)(4,1)} %get-tuple-element.249, u8[577,1024]{1,0:T(8,128)(4,1)S(1)} %get-tuple-element.248, ...), kind=kLoop, calls=%fused_computation.127 | loop fusion | flops 333238272 | bytes 30728192 | tf_op jit(solution)/shard_map/convert_element_type | solution.py:178
  1056.0 7.8 fusion.228
  1063.8 10.6 fusion.227
  1074.5 74.4 %reduce-scatter.19.cloned.1.call-done = f32[1,577,1024]{2,1,0:T(8,128)} async-done(((f32[4,577,1024]{2,1,0:T(8,128)}), f32[1,577,1024]{2,1,0:T(8,128)}) %reduce-scatter.19.cloned.1.call-update) | async-done | bytes 2363408 | tf_op jit(solution)/shard_map/reduce_scatter | solution.py:199
  1148.9 166.6 %reduce-scatter.23.cloned.1.call-done = f32[1,577,1024]{2,1,0:T(8,128)} async-done(((f32[4,577,1024]{2,1,0:T(8,128)}), f32[1,577,1024]{2,1,0:T(8,128)}) %reduce-scatter.23.cloned.1.call-update) | async-done | bytes 2363408 | tf_op jit(solution)/shard_map/reduce_scatter | solution.py:199
  1320.8 161.4 %reduce-scatter.13.cloned.1.call-done = f32[1,577,1024]{2,1,0:T(8,128)} async-done(((f32[4,577,1024]{2,1,0:T(8,128)}), f32[1,577,1024]{2,1,0:T(8,128)}) %reduce-scatter.13.cloned.1.call-update) | async-done | bytes 2363408 | tf_op jit(solution)/shard_map/reduce_scatter | solution.py:179
  1482.1 167.2 %reduce-scatter.17.cloned.1.call-done = f32[1,577,1024]{2,1,0:T(8,128)} async-done(((f32[4,577,1024]{2,1,0:T(8,128)}), f32[1,577,1024]{2,1,0:T(8,128)}) %reduce-scatter.17.cloned.1.call-update) | async-done | bytes 2363408 | tf_op jit(solution)/shard_map/reduce_scatter | solution.py:179
  1649.3 8.3 fusion.271
  1665.7 9.3 fusion.284
  1675.1 7.6 fusion.285
  1682.7 7.7 fusion.158
  1700.8 51.3 %all-gather.29.cloned.1.call-done = bf16[4,577,1024]{2,1,0:T(8,128)(2,1)} async-done(((bf16[1,577,1024]{2,1,0:T(8,128)(2,1)}), bf16[4,577,1024]{2,1,0:T(8,128)(2,1)}) %all-gather.29.cloned.1.call-update) | async-done | bytes 4726800 | tf_op jit(solution)/shard_map/all_gather | solution.py:210
  1760.1 48.8 %while.55 = (s32[]{:T(128)}, bf16[4,577,4,64]{1,3,2,0:T(8,128)(2,1)S(1)}, bf16[4,577,4,64]{1,3,2,0:T(8,128)(2,1)}, bf16[4,577,4,64]{1,3,2,0:T(8,128)(2,1)}, bf16...) while((s32[]{:T(128)}, ...), condition=%wide.region_35.36_spmd, body=%wide.region_33.35_spmd.sunk | while | flops 869015040 | bytes 49660196 | solution.py:217
  1808.9 34.2 %all-gather.25.cloned.1.call-done = bf16[4,577,1024]{2,1,0:T(8,128)(2,1)} async-done(((bf16[1,577,1024]{2,1,0:T(8,128)(2,1)}), bf16[4,577,1024]{2,1,0:T(8,128)(2,1)}) %all-gather.25.cloned.1.call-update) | async-done | bytes 4726800 | tf_op jit(solution)/shard_map/all_gather | solution.py:210
  1858.7 53.2 %while.54 = (s32[]{:T(128)}, bf16[4,577,4,64]{1,3,2,0:T(8,128)(2,1)S(1)}, bf16[4,577,4,64]{1,3,2,0:T(8,128)(2,1)}, bf16[4,577,4,64]{1,3,2,0:T(8,128)(2,1)}, bf16...) while((s32[]{:T(128)}, ...), condition=%wide.region_26.27_spmd, body=%wide.region_24.26_spmd.sunk | while | flops 869015040 | bytes 49660196 | solution.py:217
  1952.0 9.5 fusion.183
  1961.5 7.1 subtract_subtract_fusion.1
  1974.8 7.1 add_add_fusion.1
  1988.0 7.4 add_add_fusion
  1998.6 8.8 maximum_bitcast_fusion
  2025.6 79.9 %all-reduce.3.cloned.1.call-done = (f32[4,512,256]{1,2,0:T(8,128)}, f32[2,512,1024]{2,1,0:T(8,128)}) async-done(((f32[4,512,256]{1,2,0:T(8,128)}, f32[2,512,1024]{2,1,0:T(8,128)}), (f32[4,512,256]{1,2,0:T(8,128)}, f32[2,512,1024]{2,1,0:T(8,128)})) %all-reduce.3.cloned.1.call-update) | async-done | bytes 6291472 | tf_op jit(solution)/shard_map/psum | solution.py:282
  2112.1 6.6 copy.181
  2120.4 13.2 fusion.262
  2133.6 12.4 pad_maximum_fusion
  2146.0 125.0 %reduce-scatter.21.cloned.1.call-done = f32[1,577,1024]{2,1,0:T(8,128)} async-done(((f32[4,577,1024]{2,1,0:T(8,128)}), f32[1,577,1024]{2,1,0:T(8,128)}) %reduce-scatter.21.cloned.1.call-update) | async-done | bytes 2363408 | tf_op jit(solution)/shard_map/reduce_scatter | solution.py:234
  2273.4 164.4 %reduce-scatter.25.cloned.1.call-done = f32[1,577,1024]{2,1,0:T(8,128)} async-done(((f32[4,577,1024]{2,1,0:T(8,128)}), f32[1,577,1024]{2,1,0:T(8,128)}) %reduce-scatter.25.cloned.1.call-update) | async-done | bytes 2363408 | tf_op jit(solution)/shard_map/reduce_scatter | solution.py:234
  2448.6 29.2 %psum.30 = f32[12,1024]{1,0:T(8,128)S(1)} all-reduce(f32[12,1024]{1,0:T(8,128)S(1)} %concatenate.7), channel_id=1, replica_groups=mesh['group'=4,'fsdp'=2,'tensor'=4] {'fsdp','tensor'}, use_global_device_ids=true, to_apply=%region_61.62 | all-reduce | flops 12288 | bytes 98304 | tf_op jit(solution)/shard_map/psum | solution.py:272
  2477.9 17.6 psum.31
  2503.4 9.4 copy.179
  (466 shorter events, 391.5 us)
Async XLA Ops:
  7.2 16.3 all-gather.13.cloned.1.call-start
  10.1 107.3 %all-gather.19.cloned.1.call-start = ((), (), s32[]{:S(2)}) async-start(), calls=%async_computation.16 | async-start | bytes 5980160 | tf_op jit(solution)/shard_map/all_gather | solution.py:154
  19.3 189.2 %all-gather.11.cloned.1.call-start = ((), (), s32[]{:S(2)}) async-start(), calls=%async_computation.10 | async-start | bytes 5980160 | tf_op jit(solution)/shard_map/all_gather | solution.py:154
  20.0 415.1 %reduce-scatter.15.cloned.1.call-start = ((), (), s32[]{:S(2)}) async-start(), calls=%async_computation.17 | async-start | bytes 11960320 | tf_op jit(solution)/shard_map/reduce_scatter | solution.py:165
  273.1 329.1 %reduce-scatter.11.cloned.1.call-start = ((), (), s32[]{:S(2)}) async-start(), calls=%async_computation.12 | async-start | bytes 11960320 | tf_op jit(solution)/shard_map/reduce_scatter | solution.py:165
  308.4 293.9 %copy-start.65 = (f32[1,1024]{1,0:T(1,128)S(1)}, f32[1,1024]{1,0:T(1,128)}, u32[]{:S(2)}) copy-start(f32[1,1024]{1,0:T(1,128)} %get-tuple-element.393) | copy-start | bytes 12292
  308.4 320.9 %all-gather.17.cloned.1.call-start = ((), (), s32[]{:S(2)}) async-start(), calls=%async_computation.14 | async-start | bytes 6291456 | tf_op jit(solution)/shard_map/all_gather | solution.py:124
  312.3 400.3 %all-gather.21.cloned.1.call-start = ((), (), s32[]{:S(2)}) async-start(), calls=%async_computation.18 | async-start | bytes 5980160 | tf_op jit(solution)/shard_map/all_gather | solution.py:173
  609.2 194.6 %all-gather.15.cloned.1.call-start = ((), (), s32[]{:S(2)}) async-start(), calls=%async_computation.13 | async-start | bytes 5980160 | tf_op jit(solution)/shard_map/all_gather | solution.py:173
  609.9 284.4 %all-gather.23.cloned.1.call-start = ((), (), s32[]{:S(2)}) async-start(), calls=%async_computation.20 | async-start | bytes 5980160 | tf_op jit(solution)/shard_map/all_gather | solution.py:187
  623.7 361.1 %all-gather.27.cloned.1.call-start = ((), (), s32[]{:S(2)}) async-start(), calls=%async_computation.24 | async-start | bytes 5980160 | tf_op jit(solution)/shard_map/all_gather | solution.py:187
  628.2 520.7 %reduce-scatter.19.cloned.1.call-start = ((), (), s32[]{:S(2)}) async-start(), calls=%async_computation.21 | async-start | bytes 11960320 | tf_op jit(solution)/shard_map/reduce_scatter | solution.py:199
  894.3 14.5 copy-start.74
  916.9 398.6 %reduce-scatter.23.cloned.1.call-start = ((), (), s32[]{:S(2)}) async-start(), calls=%async_computation.25 | async-start | bytes 11960320 | tf_op jit(solution)/shard_map/reduce_scatter | solution.py:199
  984.7 14.7 copy-start.75
  1007.0 475.1 %reduce-scatter.13.cloned.1.call-start = ((), (), s32[]{:S(2)}) async-start(), calls=%async_computation.15 | async-start | bytes 11960320 | tf_op jit(solution)/shard_map/reduce_scatter | solution.py:179
  1007.1 48.9 %copy-start.76 = (bf16[2,1024,1024]{2,1,0:T(8,128)(2,1)S(1)}, bf16[2,1024,1024]{2,1,0:T(8,128)(2,1)}, u32[]{:S(2)}) copy-start(bf16[2,1024,1024]{2,1,0:T(8,128)(2,1)} %all-gather.17.cloned.1.call-done) | copy-start | bytes 12582916
  1063.8 585.5 %reduce-scatter.17.cloned.1.call-start = ((), (), s32[]{:S(2)}) async-start(), calls=%async_computation.19 | async-start | bytes 11960320 | tf_op jit(solution)/shard_map/reduce_scatter | solution.py:179
  1074.4 574.9 %copy-start.63 = (f32[1,1024]{1,0:T(1,128)S(1)}, f32[1,1024]{1,0:T(1,128)}, u32[]{:S(2)}) copy-start(f32[1,1024]{1,0:T(1,128)} %get-tuple-element.390) | copy-start | bytes 12292
  1074.4 677.7 %all-gather.29.cloned.1.call-start = ((), (), s32[]{:S(2)}) async-start(), calls=%async_computation.26 | async-start | bytes 5980160 | tf_op jit(solution)/shard_map/all_gather | solution.py:210
  1649.3 8.3 copy-start.8
  1660.6 182.5 %all-gather.25.cloned.1.call-start = ((), (), s32[]{:S(2)}) async-start(), calls=%async_computation.22 | async-start | bytes 5980160 | tf_op jit(solution)/shard_map/all_gather | solution.py:210
  1665.2 9.8 slice-start.2
  1665.2 286.8 %reduce-scatter.29.cloned.1.call-start = ((), (), s32[]{:S(2)}) async-start(), calls=%async_computation.29 | async-start | bytes 12582912 | tf_op jit(solution)/shard_map/reduce_scatter | solution.py:264
  1665.6 9.4 slice-start.3
  1665.7 17.0 slice-start.8
  1675.0 15.4 slice-start
  1675.1 15.4 slice-start.10
  1700.6 261.0 %reduce-scatter.27.cloned.1.call-start = ((), (), s32[]{:S(2)}) async-start(), calls=%async_computation.28 | async-start | bytes 6291456 | tf_op jit(solution)/shard_map/reduce_scatter | solution.py:263
  1937.4 168.1 %all-reduce.3.cloned.1.call-start = ((), (), s32[]{:S(2)}) async-start(), calls=%async_computation.30 | async-start | bytes 12582912 | tf_op jit(solution)/shard_map/psum | solution.py:282
  1968.6 302.4 %reduce-scatter.21.cloned.1.call-start = ((), (), s32[]{:S(2)}) async-start(), calls=%async_computation.23 | async-start | bytes 11960320 | tf_op jit(solution)/shard_map/reduce_scatter | solution.py:234
  1981.9 456.0 %reduce-scatter.25.cloned.1.call-start = ((), (), s32[]{:S(2)}) async-start(), calls=%async_computation.27 | async-start | bytes 11960320 | tf_op jit(solution)/shard_map/reduce_scatter | solution.py:234
  1998.5 8.8 copy-start.26
  1998.6 8.8 copy-start.27
  2020.1 85.3 %copy-start.17 = (f32[4,512,256]{1,2,0:T(8,128)S(1)}, f32[4,512,256]{1,2,0:T(8,128)}, u32[]{:S(2)}) copy-start(f32[4,512,256]{1,2,0:T(8,128)} %copy.172) | copy-start | bytes 6291460
  2133.6 137.4 %copy-start.4 = (bf16[1,1,1,577,1024]{4,3,2,1,0:T(8,128)(2,1)S(1)}, bf16[1,1,1,577,1024]{4,3,2,1,0:T(8,128)(2,1)}, u32[]{:S(2)}) copy-start(bf16[1,1,1,577,1024]{4,3,2,1,0:T(8,128)(2,1)} %copy-done.3) | copy-start | bytes 3545092
  2133.6 137.4 %copy-start.41 = (f32[1,1024]{1,0:T(1,128)S(1)}, f32[1,1024]{1,0:T(1,128)}, u32[]{:S(2)}) copy-start(f32[1,1024]{1,0:T(1,128)} %copy-done.40) | copy-start | bytes 12292
  2133.6 137.4 %copy-start.43 = (f32[577]{0:T(1024)S(1)}, f32[577]{0:T(1024)}, u32[]{:S(2)}) copy-start(f32[577]{0:T(1024)} %copy-done.42) | copy-start | bytes 6928
  2146.0 127.3 %copy-start.54 = (f32[577]{0:T(1024)S(1)}, f32[577]{0:T(1024)}, u32[]{:S(2)}) copy-start(f32[577]{0:T(1024)} %copy-done.53) | copy-start | bytes 6928
  2146.0 291.8 %copy-start.2 = (bf16[1,1,1,577,1024]{4,3,2,1,0:T(8,128)(2,1)S(1)}, bf16[1,1,1,577,1024]{4,3,2,1,0:T(8,128)(2,1)}, u32[]{:S(2)}) copy-start(bf16[1,1,1,577,1024]{4,3,2,1,0:T(8,128)(2,1)} %copy-done.1) | copy-start | bytes 3545092
  2146.0 291.8 %copy-start.39 = (f32[577]{0:T(1024)S(1)}, f32[577]{0:T(1024)}, u32[]{:S(2)}) copy-start(f32[577]{0:T(1024)} %copy-done.38) | copy-start | bytes 6928
  2146.0 291.8 %copy-start.49 = (f32[577]{0:T(1024)S(1)}, f32[577]{0:T(1024)}, u32[]{:S(2)}) copy-start(f32[577]{0:T(1024)} %copy-done.48) | copy-start | bytes 6928
  2273.4 168.6 %copy-start.52 = (f32[577]{0:T(1024)S(1)}, f32[577]{0:T(1024)}, u32[]{:S(2)}) copy-start(f32[577]{0:T(1024)} %copy-done.51) | copy-start | bytes 6928
  2273.4 168.7 %copy-start.47 = (f32[577]{0:T(1024)S(1)}, f32[577]{0:T(1024)}, u32[]{:S(2)}) copy-start(f32[577]{0:T(1024)} %copy-done.46) | copy-start | bytes 6928
  2273.4 168.7 %copy-start.58 = (f32[577]{0:T(1024)S(1)}, f32[577]{0:T(1024)}, u32[]{:S(2)}) copy-start(f32[577]{0:T(1024)} %copy-done.57) | copy-start | bytes 6928
  2442.4 35.4 %copy-start.35 = (f32[12,1024]{1,0:T(8,128)S(1)}, f32[12,1024]{1,0:T(8,128)}, u32[]{:S(2)}) copy-start(f32[12,1024]{1,0:T(8,128)} %param.25) | copy-start | bytes 147460
  2442.4 53.8 %copy-start.56 = (f32[577]{0:T(1024)S(1)}, f32[577]{0:T(1024)}, u32[]{:S(2)}) copy-start(f32[577]{0:T(1024)} %copy-done.55) | copy-start | bytes 6928
  2503.4 9.4 copy-start.50
  (70 other events, 297.6 us)
Sparse Core Ops, SparseCore 0:
  10.2 13.2 all-gather.12
  25.6 91.6 all-gather.18
  119.5 88.9 all-gather.10
  273.3 161.7 reduce-scatter.14
  438.0 164.2 reduce-scatter.10
  604.3 14.5 all-gather.16
  620.9 91.6 all-gather.20
  714.8 88.9 all-gather.14
  805.4 88.9 all-gather.22
  895.7 88.9 all-gather.26
  987.1 161.7 reduce-scatter.18
  1151.2 164.2 reduce-scatter.22
  1317.9 164.2 reduce-scatter.12
  1485.0 164.2 reduce-scatter.16
  1660.7 91.3 all-gather.28
  1754.1 88.9 all-gather.24
  1845.8 15.2 reduce-scatter.28
  1937.5 10.6 reduce-scatter.26
  1968.8 136.6 all-reduce.2
  2107.6 163.3 reduce-scatter.20
  2273.5 164.2 reduce-scatter.24
where the time goes:
time: 2530 us; the launch traced here: 2520 us
  waiting for transfers between devices  1800 us (71%)
  matrix products  322 us (13%)
  other arithmetic  213 us (8%)
  local copies, waits for them, and re-layouts  124 us (5%)
  blocking collectives  46.8 us (2%)
    reduce_scatter x2, waiting for transfers between devices, local(): lax.psum_scatter(jnp.einsum('isf,df->isd', hidden, mlp_all[1], preferred_...  329 us
    reduce_scatter x2, waiting for transfers between devices, local(): lax.psum_scatter(jnp.einsum('ise,de->isd', attended, attn_all[3], preferr...  290 us
    reduce_scatter x2, waiting for transfers between devices, local(): lax.psum_scatter(summed + jnp.einsum('ise,de->isd', grad_values, attn_all...  289 us
    reduce_scatter x2, waiting for transfers between devices, local(): lax.psum_scatter(jnp.einsum('isf,df->isd', grad_pre, mlp_all[0], preferre...  241 us
    all_gather x2, waiting for transfers between devices, local(): rows_attn = lax.all_gather(normed_one, 'tensor', axis=0, tiled=True)  176 us
    all_gather x2, waiting for transfers between devices, local(): rows_mlp = lax.all_gather(normed_two, 'tensor', axis=0, tiled=True)  164 us
    all_gather x2, waiting for transfers between devices, local(): lax.all_gather(grad_out.astype(narrow), 'tensor', axis=0, tiled=True)  138 us
    all_gather x2, waiting for transfers between devices, local(): lax.all_gather(grad_resid.astype(narrow), 'tensor', axis=0, tiled=True)  85.5 us
  transfers between devices with their start and end apart: 21, of which 18 were waited for; matrix products, arithmetic and copies ran while one was open for 21% of the time, Pallas kernels for 0%

commit v1 on v0

--- a/solution.py
+++ b/solution.py
@@ -13,6 +13,35 @@
 WEIGHT_DECAY = 0.1
 OUTER_RATE = 0.7
 OUTER_MOMENTUM = 0.9
+
+
+def plan_loops(panel, dim_no):
+    panel = jnp.moveaxis(panel, 0, dim_no)
+    carry_out = panel.shape
+    taken_in = panel.reshape(
+        *carry_out[:dim_no], carry_out[dim_no] * carry_out[dim_no + 1], *carry_out[dim_no + 2 :]
+    )
+    return taken_in
+
+
+def _press_types(load, across):
+    field_out = lax.axis_size(across)
+    w1, r1 = (field_out, lax.axis_index(across))
+    step_out, e_next = (load[None], 1)
+    while e_next < w1:
+        raw_out = lax.ppermute(step_out, across, [(i0, i0 ^ e_next) for i0 in range(w1)])
+        current_arr = r1 & e_next == 0
+        step_out = jnp.concatenate(
+            [jnp.where(current_arr, step_out, raw_out), jnp.where(current_arr, raw_out, step_out)]
+        )
+        e_next *= 2
+    return step_out
+
+
+def launch_digits_up(obj, local_array, d0):
+    arr_next = _press_types(obj, local_array)
+    high = plan_loops(arr_next, d0)
+    return high
 
 
 def normalize(source, gain_row, shift_row):
@@ -184,7 +213,7 @@
         )
         outputs_mixed.append((alive * (resid_one + branch_two + vector_master[7])).astype(narrow))
         grad_out = alive * output_grad[0, batch_index].astype(single)
-        rows_grad_two = lax.all_gather(grad_out.astype(narrow), "tensor", axis=0, tiled=True)
+        rows_grad_two = launch_digits_up(grad_out.astype(narrow), "tensor", d0=0)
         fc_out_acc = fc_out_acc + jnp.einsum(
             "isd,isf->df", rows_grad_two, hidden, preferred_element_type=single
         )

time: 2530 us -> 2620 us (1.036)
  waiting for transfers between devices: 1800 us -> 1870 us
    ppermute x0 -> x4, waiting for transfers between devices: none -> 525 us  [_press_types(): lax.ppermute(step_out, across, [(i0, i0 ^ e_next) for i0 in range(w1)])]
    all_gather x2, waiting for transfers between devices: 164 us -> 0.01 us  [local(): rows_mlp = lax.all_gather(normed_two, 'tensor', axis=0, tiled=True)]
    reduce_scatter x2, waiting for transfers between devices: 241 us -> 94.8 us  [local(): lax.psum_scatter(jnp.einsum('isf,df->isd', grad_pre, mlp_all[0], preferre...]
    all_gather x2 -> x0, waiting for transfers between devices: 138 us -> none  [local(): lax.all_gather(grad_out.astype(narrow), 'tensor', axis=0, tiled=True)]
  transfers between devices with their start and end apart: 21 -> 23, of which waited for: 18 -> 17; matrix products, arithmetic and copies ran while one was open for 21% -> 21% of each run, Pallas kernels for 0% -> 0%
where the time goes in v1:
time: 2620 us; the launch traced here: 2610 us
  waiting for transfers between devices  1870 us (71%)
  matrix products  320 us (12%)
  other arithmetic  227 us (9%)
  local copies, waits for them, and re-layouts  129 us (5%)
  blocking collectives  46.8 us (2%)
    ppermute x4, waiting for transfers between devices, _press_types(): lax.ppermute(step_out, across, [(i0, i0 ^ e_next) for i0 in range(w1)])  525 us
    reduce_scatter x2, waiting for transfers between devices, local(): lax.psum_scatter(jnp.einsum('isf,df->isd', hidden, mlp_all[1], preferred_...  329 us
    reduce_scatter x2, waiting for transfers between devices, local(): lax.psum_scatter(jnp.einsum('ise,de->isd', attended, attn_all[3], preferr...  290 us
    reduce_scatter x2, waiting for transfers between devices, local(): lax.psum_scatter(summed + jnp.einsum('ise,de->isd', grad_values, attn_all...  290 us
    all_gather x2, waiting for transfers between devices, local(): rows_attn = lax.all_gather(normed_one, 'tensor', axis=0, tiled=True)  176 us
    reduce_scatter x2, waiting for transfers between devices, local(): lax.psum_scatter(jnp.einsum('isf,df->isd', grad_pre, mlp_all[0], preferre...  94.8 us
    all_gather x2, waiting for transfers between devices, local(): lax.all_gather(grad_resid.astype(narrow), 'tensor', axis=0, tiled=True)  83.2 us
    psum x1, waiting for transfers between devices, local(): lax.psum((attn_master - new_attn, mlp_master - new_mlp, vector_master - n...  79.8 us
  transfers between devices with their start and end apart: 23, of which 17 were waited for; matrix products, arithmetic and copies ran while one was open for 21% of the time, Pallas kernels for 0%

profile of v1, /device:TPU:0, one launch (start us, length us, event | category | flops | bytes accessed | tf_op | source)
XLA Modules:
  0.0 2614.9 jit_solution(1135461553674260278)
XLA Ops:
  23.5 93.8 %all-gather.17.cloned.1.call-done = bf16[4,577,1024]{2,1,0:T(8,128)(2,1)} async-done(((bf16[1,577,1024]{2,1,0:T(8,128)(2,1)}), bf16[4,577,1024]{2,1,0:T(8,128)(2,1)}) %all-gather.17.cloned.1.call-update) | async-done | bytes 4726800 | tf_op jit(solution)/shard_map/all_gather | solution.py:183
  126.6 81.9 %all-gather.9.cloned.1.call-done = bf16[4,577,1024]{2,1,0:T(8,128)(2,1)} async-done(((bf16[1,577,1024]{2,1,0:T(8,128)(2,1)}), bf16[4,577,1024]{2,1,0:T(8,128)(2,1)}) %all-gather.9.cloned.1.call-update) | async-done | bytes 4726800 | tf_op jit(solution)/shard_map/all_gather | solution.py:183
  208.5 6.4 fusion.186
  240.4 25.3 while.53
  265.7 7.3 fusion.243
  279.2 21.5 while.52
  300.6 7.9 fusion.244
  312.6 122.5 %reduce-scatter.15.cloned.1.call-done = f32[1,577,1024]{2,1,0:T(8,128)} async-done(((f32[4,577,1024]{2,1,0:T(8,128)}), f32[1,577,1024]{2,1,0:T(8,128)}) %reduce-scatter.15.cloned.1.call-update) | async-done | bytes 2363408 | tf_op jit(solution)/shard_map/reduce_scatter | solution.py:194
  435.1 167.2 %reduce-scatter.11.cloned.1.call-done = f32[1,577,1024]{2,1,0:T(8,128)} async-done(((f32[4,577,1024]{2,1,0:T(8,128)}), f32[1,577,1024]{2,1,0:T(8,128)}) %reduce-scatter.11.cloned.1.call-update) | async-done | bytes 2363408 | tf_op jit(solution)/shard_map/reduce_scatter | solution.py:194
  610.9 7.1 fusion.289
  626.1 66.2 %collective-permute-done = bf16[1,1,577,1024]{3,2,1,0:T(8,128)(2,1)} collective-permute-done((bf16[1,1,577,1024]{3,2,1,0:T(8,128)(2,1)}, bf16[1,1,577,1024]{3,2,1,0:T(8,128)(2,1)}, u32[]{:S(2)}, u32[]{:S(2)}) %collective-permute-start) | collective-permute-done | bytes 1181728 | tf_op jit(solution)/shard_map/ppermute | solution.py:32
  692.3 59.3 %collective-permute-done.2 = bf16[1,1,577,1024]{3,2,1,0:T(8,128)(2,1)} collective-permute-done((bf16[1,1,577,1024]{3,2,1,0:T(8,128)(2,1)}, bf16[1,1,577,1024]{3,2,1,0:T(8,128)(2,1)}, u32[]{:S(2)}, u32[]{:S(2)}) %collective-permute-start.2) | collective-permute-done | bytes 1181728 | tf_op jit(solution)/shard_map/ppermute | solution.py:32
  763.6 178.1 %collective-permute-done.3 = bf16[2,1,577,1024]{3,0,2,1:T(2,128)(2,1)} collective-permute-done((bf16[2,1,577,1024]{3,0,2,1:T(2,128)(2,1)}, bf16[2,1,577,1024]{3,0,2,1:T(2,128)(2,1)}, u32[]{:S(2)}, u32[]{:S(2)}) %collective-permute-start.3) | collective-permute-done | bytes 2363424 | tf_op jit(solution)/shard_map/ppermute | solution.py:32
  947.2 8.0 fusion.229
  955.3 9.7 convert_reduce_fusion
  967.1 7.9 fusion.227
  979.5 221.1 %collective-permute-done.1 = bf16[2,1,577,1024]{3,0,2,1:T(2,128)(2,1)S(1)} collective-permute-done((bf16[2,1,577,1024]{3,0,2,1:T(2,128)(2,1)S(1)}, bf16[2,1,577,1024]{3,0,2,1:T(2,128)(2,1)S(1)}, u32[]{:S(2)}, u32[]{:S(2)}) %collective-permute-start.1) | collective-permute-done | bytes 2363424 | tf_op jit(solution)/shard_map/ppermute | solution.py:32
  1203.8 19.4 fusion.214
  1223.2 14.0 convert_reduce_fusion.1
  1239.4 7.8 fusion.228
  1247.2 46.9 %fusion.116 = (bf16[4,577,1024]{2,1,0:T(8,128)(2,1)S(1)}, bf16[4,577,1024]{2,1,0:T(8,128)(2,1)}) fusion(f32[4,577,1024]{2,1,0:T(8,128)} %copy-done.28, f32[1024]{0:T(1024)S(1)} %dynamic_slice.61, u8[577,1024]{1,0:T(8,128)(4,1)} %get-tuple-element.249, u8[577,1024]{1,0:T(8,128)(4,1)S(1)} %get-tuple-element.248, u8[577,1024]{1,0:T(8,128)(4,1)} %get-tuple-element.266, ...), kind=kLoop, calls=%fused_computation.127 | loop fusion | flops 333238272 | bytes 30728192 | tf_op jit(solution)/shard_map/convert_element_type | solution.py:207
  1296.3 7.8 fusion.232
  1304.1 10.4 fusion.231
  1314.8 94.8 %reduce-scatter.19.cloned.1.call-done = f32[1,577,1024]{2,1,0:T(8,128)} async-done(((f32[4,577,1024]{2,1,0:T(8,128)}), f32[1,577,1024]{2,1,0:T(8,128)}) %reduce-scatter.19.cloned.1.call-update) | async-done | bytes 2363408 | tf_op jit(solution)/shard_map/reduce_scatter | solution.py:228
  1414.8 161.4 %reduce-scatter.13.cloned.1.call-done = f32[1,577,1024]{2,1,0:T(8,128)} async-done(((f32[4,577,1024]{2,1,0:T(8,128)}), f32[1,577,1024]{2,1,0:T(8,128)}) %reduce-scatter.13.cloned.1.call-update) | async-done | bytes 2363408 | tf_op jit(solution)/shard_map/reduce_scatter | solution.py:208
  1576.2 167.2 %reduce-scatter.17.cloned.1.call-done = f32[1,577,1024]{2,1,0:T(8,128)} async-done(((f32[4,577,1024]{2,1,0:T(8,128)}), f32[1,577,1024]{2,1,0:T(8,128)}) %reduce-scatter.17.cloned.1.call-update) | async-done | bytes 2363408 | tf_op jit(solution)/shard_map/reduce_scatter | solution.py:208
  1743.4 8.3 fusion.281
  1759.3 10.5 fusion.172
  1769.9 9.0 fusion.294
  1779.0 7.8 fusion.157
  1797.1 49.1 %all-gather.23.cloned.1.call-done = bf16[4,577,1024]{2,1,0:T(8,128)(2,1)} async-done(((bf16[1,577,1024]{2,1,0:T(8,128)(2,1)}), bf16[4,577,1024]{2,1,0:T(8,128)(2,1)}) %all-gather.23.cloned.1.call-update) | async-done | bytes 4726800 | tf_op jit(solution)/shard_map/all_gather | solution.py:239
  1854.4 48.7 %while.55 = (s32[]{:T(128)}, bf16[4,577,4,64]{1,3,2,0:T(8,128)(2,1)S(1)}, bf16[4,577,4,64]{1,3,2,0:T(8,128)(2,1)}, bf16[4,577,4,64]{1,3,2,0:T(8,128)(2,1)}, bf16...) while((s32[]{:T(128)}, ...), condition=%wide.region_35.36_spmd, body=%wide.region_33.35_spmd.sunk | while | flops 869015040 | bytes 49660196 | solution.py:246
  1903.1 34.1 %all-gather.21.cloned.1.call-done = bf16[4,577,1024]{2,1,0:T(8,128)(2,1)} async-done(((bf16[1,577,1024]{2,1,0:T(8,128)(2,1)}), bf16[4,577,1024]{2,1,0:T(8,128)(2,1)}) %all-gather.21.cloned.1.call-update) | async-done | bytes 4726800 | tf_op jit(solution)/shard_map/all_gather | solution.py:239
  1952.7 53.4 %while.54 = (s32[]{:T(128)}, bf16[4,577,4,64]{1,3,2,0:T(8,128)(2,1)S(1)}, bf16[4,577,4,64]{1,3,2,0:T(8,128)(2,1)}, bf16[4,577,4,64]{1,3,2,0:T(8,128)(2,1)}, bf16...) while((s32[]{:T(128)}, ...), condition=%wide.region_26.27_spmd, body=%wide.region_24.26_spmd.sunk | while | flops 869015040 | bytes 49660196 | solution.py:246
  2046.0 9.5 fusion.185
  2055.6 7.1 subtract_subtract_fusion.1
  2068.8 7.0 add_add_fusion.1
  2082.3 7.3 add_add_fusion
  2092.8 8.8 maximum_bitcast_fusion
  2119.7 79.8 %all-reduce.3.cloned.1.call-done = (f32[4,512,256]{1,2,0:T(8,128)}, f32[2,512,1024]{2,1,0:T(8,128)}) async-done(((f32[4,512,256]{1,2,0:T(8,128)}, f32[2,512,1024]{2,1,0:T(8,128)}), (f32[4,512,256]{1,2,0:T(8,128)}, f32[2,512,1024]{2,1,0:T(8,128)})) %all-reduce.3.cloned.1.call-update) | async-done | bytes 6291472 | tf_op jit(solution)/shard_map/psum | solution.py:311
  2206.2 6.6 copy.187
  2214.3 13.2 fusion.272
  2227.5 12.4 pad_maximum_fusion
  2239.9 125.3 %reduce-scatter.21.cloned.1.call-done = f32[1,577,1024]{2,1,0:T(8,128)} async-done(((f32[4,577,1024]{2,1,0:T(8,128)}), f32[1,577,1024]{2,1,0:T(8,128)}) %reduce-scatter.21.cloned.1.call-update) | async-done | bytes 2363408 | tf_op jit(solution)/shard_map/reduce_scatter | solution.py:263
  2367.5 164.4 %reduce-scatter.25.cloned.1.call-done = f32[1,577,1024]{2,1,0:T(8,128)} async-done(((f32[4,577,1024]{2,1,0:T(8,128)}), f32[1,577,1024]{2,1,0:T(8,128)}) %reduce-scatter.25.cloned.1.call-update) | async-done | bytes 2363408 | tf_op jit(solution)/shard_map/reduce_scatter | solution.py:263
  2542.6 29.2 %psum.30 = f32[12,1024]{1,0:T(8,128)S(1)} all-reduce(f32[12,1024]{1,0:T(8,128)S(1)} %concatenate.23), channel_id=1, replica_groups=mesh['group'=4,'fsdp'=2,'tensor'=4] {'fsdp','tensor'}, use_global_device_ids=true, to_apply=%region_61.62 | all-reduce | flops 12288 | bytes 98304 | tf_op jit(solution)/shard_map/psum | solution.py:301
  2571.9 17.6 psum.31
  2597.4 9.4 copy.185
  (499 shorter events, 408.1 us)
Async XLA Ops:
  7.2 16.3 all-gather.11.cloned.1.call-start
  10.1 107.3 %all-gather.17.cloned.1.call-start = ((), (), s32[]{:S(2)}) async-start(), calls=%async_computation.16 | async-start | bytes 5980160 | tf_op jit(solution)/shard_map/all_gather | solution.py:183
  18.8 189.7 %all-gather.9.cloned.1.call-start = ((), (), s32[]{:S(2)}) async-start(), calls=%async_computation.10 | async-start | bytes 5980160 | tf_op jit(solution)/shard_map/all_gather | solution.py:183
  19.5 415.6 %reduce-scatter.15.cloned.1.call-start = ((), (), s32[]{:S(2)}) async-start(), calls=%async_computation.17 | async-start | bytes 11960320 | tf_op jit(solution)/shard_map/reduce_scatter | solution.py:194
  273.1 329.1 %reduce-scatter.11.cloned.1.call-start = ((), (), s32[]{:S(2)}) async-start(), calls=%async_computation.12 | async-start | bytes 11960320 | tf_op jit(solution)/shard_map/reduce_scatter | solution.py:194
  308.6 293.7 %copy-start.76 = (f32[1,1024]{1,0:T(1,128)S(1)}, f32[1,1024]{1,0:T(1,128)}, u32[]{:S(2)}) copy-start(f32[1,1024]{1,0:T(1,128)} %get-tuple-element.401) | copy-start | bytes 12292
  308.6 638.6 %all-gather.15.cloned.1.call-start = ((), (), s32[]{:S(2)}) async-start(), calls=%async_computation.14 | async-start | bytes 6291456 | tf_op jit(solution)/shard_map/all_gather | solution.py:153
  312.5 634.7 %all-gather.19.cloned.1.call-start = ((), (), s32[]{:S(2)}) async-start(), calls=%async_computation.18 | async-start | bytes 5980160 | tf_op jit(solution)/shard_map/all_gather | solution.py:202
  609.7 594.1 %all-gather.13.cloned.1.call-start = ((), (), s32[]{:S(2)}) async-start(), calls=%async_computation.13 | async-start | bytes 5980160 | tf_op jit(solution)/shard_map/all_gather | solution.py:202
  621.2 71.2 %collective-permute-start = (bf16[1,1,577,1024]{3,2,1,0:T(8,128)(2,1)}, bf16[1,1,577,1024]{3,2,1,0:T(8,128)(2,1)}, u32[]{:S(2)}, u32[]{:S(2)}) collective-permute-start(bf16[1,1,577,1024]{3,2,1,0:T(8,128)(2,1)} %get-tuple-element.384), channel_id=1, source_target_pairs={{0,1},{1,0},{2,3},{3,2},{4,5},{5,4},{6,7},{7,6},{8,9},{9,8},{10,11... | collective-permute-start | bytes 3545096 | tf_op jit(solution)/shard_map/ppermute | solution.py:32
  625.3 126.3 %collective-permute-start.2 = (bf16[1,1,577,1024]{3,2,1,0:T(8,128)(2,1)}, bf16[1,1,577,1024]{3,2,1,0:T(8,128)(2,1)}, u32[]{:S(2)}, u32[]{:S(2)}) collective-permute-start(bf16[1,1,577,1024]{3,2,1,0:T(8,128)(2,1)} %get-tuple-element.382), channel_id=1, source_target_pairs={{0,1},{1,0},{2,3},{3,2},{4,5},{5,4},{6,7},{7,6},{8,9},{9,8},{10,11... | collective-permute-start | bytes 3545096 | tf_op jit(solution)/shard_map/ppermute | solution.py:32
  626.1 688.7 %reduce-scatter.23.cloned.1.call-start = ((), (), s32[]{:S(2)}) async-start(), calls=%async_computation.23 | async-start | bytes 11960320 | tf_op jit(solution)/shard_map/reduce_scatter | solution.py:228
  761.2 180.5 %collective-permute-start.3 = (bf16[2,1,577,1024]{3,0,2,1:T(2,128)(2,1)}, bf16[2,1,577,1024]{3,0,2,1:T(2,128)(2,1)}, u32[]{:S(2)}, u32[]{:S(2)}) collective-permute-start(bf16[2,1,577,1024]{3,0,2,1:T(2,128)(2,1)} %copy.157), channel_id=1, source_target_pairs={{0,2},{1,3},{2,0},{3,1},{4,6},{5,7},{6,4},{7,5},{8,10},{9,11},{10,... | collective-permute-start | bytes 7090184 | tf_op jit(solution)/shard_map/ppermute | solution.py:32
  975.1 434.5 %reduce-scatter.19.cloned.1.call-start = ((), (), s32[]{:S(2)}) async-start(), calls=%async_computation.20 | async-start | bytes 11960320 | tf_op jit(solution)/shard_map/reduce_scatter | solution.py:228
  977.0 223.6 %copy-start.21 = (bf16[1,1,577,1024]{3,2,1,0:T(8,128)(2,1)S(1)}, bf16[1,1,577,1024]{3,2,1,0:T(8,128)(2,1)}, u32[]{:S(2)}) copy-start(bf16[1,1,577,1024]{3,2,1,0:T(8,128)(2,1)} %get-tuple-element.438) | copy-start | bytes 3545092
  977.0 223.6 %copy-start.22 = (bf16[1,1,577,1024]{3,2,1,0:T(8,128)(2,1)S(1)}, bf16[1,1,577,1024]{3,2,1,0:T(8,128)(2,1)}, u32[]{:S(2)}) copy-start(bf16[1,1,577,1024]{3,2,1,0:T(8,128)(2,1)} %get-tuple-element.439) | copy-start | bytes 3545092
  979.4 221.2 %collective-permute-start.1 = (bf16[2,1,577,1024]{3,0,2,1:T(2,128)(2,1)S(1)}, bf16[2,1,577,1024]{3,0,2,1:T(2,128)(2,1)S(1)}, u32[]{:S(2)}, u32[]{:S(2)}) collective-permute-start(bf16[2,1,577,1024]{3,0,2,1:T(2,128)(2,1)S(1)} %copy.149), channel_id=1, source_target_pairs={{0,2},{1,3},{2,0},{3,1},{4,6},{5,7},{6,4},{7,5},{8,10},{9,11},{10,... | collective-permute-start | bytes 7090184 | tf_op jit(solution)/shard_map/ppermute | solution.py:32
  1223.2 14.0 copy-start.28
  1223.2 16.2 copy-start.86
  1247.2 329.0 %reduce-scatter.13.cloned.1.call-start = ((), (), s32[]{:S(2)}) async-start(), calls=%async_computation.15 | async-start | bytes 11960320 | tf_op jit(solution)/shard_map/reduce_scatter | solution.py:208
  1247.2 49.1 %copy-start.87 = (bf16[2,1024,1024]{2,1,0:T(8,128)(2,1)S(1)}, bf16[2,1024,1024]{2,1,0:T(8,128)(2,1)}, u32[]{:S(2)}) copy-start(bf16[2,1024,1024]{2,1,0:T(8,128)(2,1)} %all-gather.15.cloned.1.call-done) | copy-start | bytes 12582916
  1304.1 439.3 %reduce-scatter.17.cloned.1.call-start = ((), (), s32[]{:S(2)}) async-start(), calls=%async_computation.19 | async-start | bytes 11960320 | tf_op jit(solution)/shard_map/reduce_scatter | solution.py:208
  1314.5 428.8 %copy-start.74 = (f32[1,1024]{1,0:T(1,128)S(1)}, f32[1,1024]{1,0:T(1,128)}, u32[]{:S(2)}) copy-start(f32[1,1024]{1,0:T(1,128)} %get-tuple-element.398) | copy-start | bytes 12292
  1314.5 531.6 %all-gather.23.cloned.1.call-start = ((), (), s32[]{:S(2)}) async-start(), calls=%async_computation.24 | async-start | bytes 5980160 | tf_op jit(solution)/shard_map/all_gather | solution.py:239
  1754.7 182.5 %all-gather.21.cloned.1.call-start = ((), (), s32[]{:S(2)}) async-start(), calls=%async_computation.21 | async-start | bytes 5980160 | tf_op jit(solution)/shard_map/all_gather | solution.py:239
  1754.7 15.1 slice-start.8
  1759.2 286.8 %reduce-scatter.29.cloned.1.call-start = ((), (), s32[]{:S(2)}) async-start(), calls=%async_computation.27 | async-start | bytes 12582912 | tf_op jit(solution)/shard_map/reduce_scatter | solution.py:293
  1759.3 10.6 slice-start.9
  1759.3 19.6 slice-start
  1769.9 17.0 slice-start.6
  1769.9 17.0 slice-start.10
  1797.0 258.5 %reduce-scatter.27.cloned.1.call-start = ((), (), s32[]{:S(2)}) async-start(), calls=%async_computation.26 | async-start | bytes 6291456 | tf_op jit(solution)/shard_map/reduce_scatter | solution.py:292
  2031.3 168.2 %all-reduce.3.cloned.1.call-start = ((), (), s32[]{:S(2)}) async-start(), calls=%async_computation.28 | async-start | bytes 12582912 | tf_op jit(solution)/shard_map/psum | solution.py:311
  2062.7 302.5 %reduce-scatter.21.cloned.1.call-start = ((), (), s32[]{:S(2)}) async-start(), calls=%async_computation.22 | async-start | bytes 11960320 | tf_op jit(solution)/shard_map/reduce_scatter | solution.py:263
  2075.9 456.0 %reduce-scatter.25.cloned.1.call-start = ((), (), s32[]{:S(2)}) async-start(), calls=%async_computation.25 | async-start | bytes 11960320 | tf_op jit(solution)/shard_map/reduce_scatter | solution.py:263
  2114.3 85.2 %copy-start.18 = (f32[4,512,256]{1,2,0:T(8,128)S(1)}, f32[4,512,256]{1,2,0:T(8,128)}, u32[]{:S(2)}) copy-start(f32[4,512,256]{1,2,0:T(8,128)} %copy.178) | copy-start | bytes 6291460
  2227.5 137.7 %copy-start.4 = (bf16[1,1,1,577,1024]{4,3,2,1,0:T(8,128)(2,1)S(1)}, bf16[1,1,1,577,1024]{4,3,2,1,0:T(8,128)(2,1)}, u32[]{:S(2)}) copy-start(bf16[1,1,1,577,1024]{4,3,2,1,0:T(8,128)(2,1)} %copy-done.3) | copy-start | bytes 3545092
  2227.5 137.7 %copy-start.52 = (f32[1,1024]{1,0:T(1,128)S(1)}, f32[1,1024]{1,0:T(1,128)}, u32[]{:S(2)}) copy-start(f32[1,1024]{1,0:T(1,128)} %copy-done.51) | copy-start | bytes 12292
  2227.5 137.7 %copy-start.54 = (f32[577]{0:T(1024)S(1)}, f32[577]{0:T(1024)}, u32[]{:S(2)}) copy-start(f32[577]{0:T(1024)} %copy-done.53) | copy-start | bytes 6928
  2239.9 127.6 %copy-start.65 = (f32[577]{0:T(1024)S(1)}, f32[577]{0:T(1024)}, u32[]{:S(2)}) copy-start(f32[577]{0:T(1024)} %copy-done.64) | copy-start | bytes 6928
  2239.9 292.0 %copy-start.2 = (bf16[1,1,1,577,1024]{4,3,2,1,0:T(8,128)(2,1)S(1)}, bf16[1,1,1,577,1024]{4,3,2,1,0:T(8,128)(2,1)}, u32[]{:S(2)}) copy-start(bf16[1,1,1,577,1024]{4,3,2,1,0:T(8,128)(2,1)} %copy-done.1) | copy-start | bytes 3545092
  2239.9 292.0 %copy-start.50 = (f32[577]{0:T(1024)S(1)}, f32[577]{0:T(1024)}, u32[]{:S(2)}) copy-start(f32[577]{0:T(1024)} %copy-done.49) | copy-start | bytes 6928
  2239.9 292.0 %copy-start.60 = (f32[577]{0:T(1024)S(1)}, f32[577]{0:T(1024)}, u32[]{:S(2)}) copy-start(f32[577]{0:T(1024)} %copy-done.59) | copy-start | bytes 6928
  2367.4 168.6 %copy-start.63 = (f32[577]{0:T(1024)S(1)}, f32[577]{0:T(1024)}, u32[]{:S(2)}) copy-start(f32[577]{0:T(1024)} %copy-done.62) | copy-start | bytes 6928
  2367.4 168.7 %copy-start.58 = (f32[577]{0:T(1024)S(1)}, f32[577]{0:T(1024)}, u32[]{:S(2)}) copy-start(f32[577]{0:T(1024)} %copy-done.57) | copy-start | bytes 6928
  2367.5 168.7 %copy-start.69 = (f32[577]{0:T(1024)S(1)}, f32[577]{0:T(1024)}, u32[]{:S(2)}) copy-start(f32[577]{0:T(1024)} %copy-done.68) | copy-start | bytes 6928
  2536.5 35.3 %copy-start.46 = (f32[12,1024]{1,0:T(8,128)S(1)}, f32[12,1024]{1,0:T(8,128)}, u32[]{:S(2)}) copy-start(f32[12,1024]{1,0:T(8,128)} %param.25) | copy-start | bytes 147460
  2536.5 53.7 %copy-start.67 = (f32[577]{0:T(1024)S(1)}, f32[577]{0:T(1024)}, u32[]{:S(2)}) copy-start(f32[577]{0:T(1024)} %copy-done.66) | copy-start | bytes 6928
  (84 other events, 404.3 us)
Sparse Core Ops, SparseCore 0:
  10.2 13.2 all-gather.10
  25.6 91.6 all-gather.16
  119.5 88.9 all-gather.8
  273.2 161.7 reduce-scatter.14
  438.0 164.2 reduce-scatter.10
  604.2 14.5 all-gather.14
  620.9 130.0 all-gather.18
  753.1 178.3 all-gather.12
  975.2 255.0 reduce-scatter.22
  1247.3 162.2 reduce-scatter.18
  1411.9 164.2 reduce-scatter.12
  1579.1 164.2 reduce-scatter.16
  1754.8 91.3 all-gather.22
  1848.2 88.9 all-gather.20
  1939.9 15.2 reduce-scatter.28
  2031.4 10.6 reduce-scatter.26
  2062.8 136.6 all-reduce.2
  2201.7 163.3 reduce-scatter.20
  2367.6 164.2 reduce-scatter.24
